TPU v7x, 32 devices: a whole 2x2x4 slice. The times are simulated.
32 devices in a mesh: gx: 16 (over z, y, core), gy: 2 (over x).
Axes of the slice: x: 2, y: 2, z: 4, core: 2. Of those that a mesh axis runs over, the one named last changes fastest.
Arguments:
- right_side: float32 [16, 2, 512, 256], P('gx', 'gy'), may hold values from -8 to 8, as said below
- coords: float32 [16, 2, 2, 512], P('gx', 'gy'), may hold values from 0 to 1
- noise: float32 [16, 2, 512], P('gx', 'gy'), may hold values from 0.25 to 1
- intersect: int32 [16, 2, 128], P('gx', 'gy'), may hold values from 0 to 4607, as said below
Outputs:
- solution: float32 [16, 2, 512, 256], P('gx', 'gy')
- residual: float32 [16, 2, 512, 256], P('gx', 'gy')
Inputs may be any that keep to these rules, and one draw needn't show every extreme that they name: `right_side`: right-hand sides of order one. `intersect`: each subdomain's list holds 128 distinct indices in increasing order; none names the subdomain itself (block number 4) or a subdomain beyond the first or last one along the second dimension.
All inputs are finite; a program needn't handle non-finite values.
Results may differ from a plain program's by a relative error of at most 0.0003.
Values sent between devices are 32-bit elements; how exact they have to be, the bound alone decides.
A program may use at most 128 MiB of HBM per device.

v0:
```python
import math
import jax
import jax.numpy as jnp
from jax import lax
from jax.sharding import PartitionSpec as P

ITERS = 3
RANGE_LEN = 0.25
ROOT_THREE = math.sqrt(3.0)
HIGH = lax.Precision.HIGHEST


def shifted(value, axis, by):
    count = lax.axis_size(axis)
    return lax.ppermute(value, axis, [(i, (i + by) % count) for i in range(count)])


def passed_along(block, axis, distance):
    devices = range(lax.axis_size(axis))
    route = [(i - distance, i) for i in devices if i - distance in devices]
    return lax.ppermute(block, axis, route)


def kernel_block(rows_pos, cols_pos):
    delta_x = rows_pos[0][:, None] - cols_pos[0][None, :]
    delta_y = rows_pos[1][:, None] - cols_pos[1][None, :]
    distance = jnp.sqrt(delta_x * delta_x + delta_y * delta_y)
    scaled = ROOT_THREE / RANGE_LEN * distance
    clipped = jnp.minimum(distance, 1.0)
    taper_val = jnp.square(jnp.square(1.0 - clipped)) * (4.0 * clipped + 1.0)
    return (1.0 + scaled) * jnp.exp(-scaled) * taper_val


def window_values(values):
    beside = {}
    for step_by in (1, -1):
        beside[step_by] = shifted(values, "gx", step_by)
    column = jnp.stack([beside[1], values, beside[-1]])
    across = {}
    for step_by in (1, -1):
        across[step_by] = passed_along(column, "gy", step_by)
    return [across[1], column, across[-1]]


def window_index(values):
    beside = {}
    for step_by in (1, -1):
        beside[step_by] = shifted(values, "gx", step_by)
    column = jnp.stack([beside[1], values, beside[-1]])
    across = {}
    for step_by in (1, -1):
        across[step_by] = passed_along(column, "gy", step_by)
    return [across[1], column, across[-1]]


def column_sum(first, second):
    return jnp.sum(first * second, axis=0)


def residual_dot(residue, precond):
    return lax.psum(column_sum(residue, precond), ("gx", "gy"))


def shards(right_side, coords, noise, intersect):
    points = right_side.shape[2]
    rhs_count = right_side.shape[3]
    intersect_len = intersect.shape[2]
    ext_len = points + intersect_len
    own_pos = coords.reshape(2, points)
    own_noise = noise.reshape(points)
    point_info = jnp.concatenate([own_pos, own_noise[None, :]], axis=0)
    info_cols = window_values(point_info)
    positions = [
        [
            jnp.stack(
                [
                    info_cols[col_off][row_off, 0] + float(row_off - 1),
                    info_cols[col_off][row_off, 1] + float(col_off - 1),
                ]
            )
            for col_off in range(3)
        ]
        for row_off in range(3)
    ]
    intersect_ids = intersect.reshape(intersect_len)
    block_id = intersect_ids // points
    row_in = intersect_ids % points
    row_of = block_id // 3
    col_of = block_id % 3
    local_id = row_of * points + row_in
    picked_info = [
        jnp.take(
            jnp.transpose(info_cols[col_off], (1, 0, 2)).reshape(3, 3 * points), local_id, axis=1
        )
        for col_off in range(3)
    ]
    chosen = jnp.where(
        col_of[None, :] == 0,
        picked_info[0],
        jnp.where(col_of[None, :] == 1, picked_info[1], picked_info[2]),
    )
    ov_pos = jnp.stack(
        [chosen[0] + (row_of - 1).astype(jnp.float32), chosen[1] + (col_of - 1).astype(jnp.float32)]
    )
    ext_pos = jnp.concatenate([own_pos, ov_pos], axis=1)
    ext_noise = jnp.concatenate([own_noise, chosen[2]])
    local_matrix = kernel_block(ext_pos, ext_pos) + jnp.diag(ext_noise)
    factor = jnp.linalg.cholesky(local_matrix)
    inv_factor = lax.linalg.triangular_solve(
        factor, jnp.eye(ext_len, dtype=jnp.float32), left_side=True, lower=True
    )
    inverse = jnp.dot(inv_factor.T, inv_factor, precision=HIGH, preferred_element_type=jnp.float32)
    near_ids = window_index(intersect_ids)
    point_iota = jnp.arange(points, dtype=jnp.int32)[:, None]
    row_base = (2 - jnp.arange(3, dtype=jnp.int32))[:, None] * 3
    selectors = []
    for col_off in range(3):
        own_rows = near_ids[col_off] - (row_base + (2 - col_off)) * points
        selectors.append((point_iota == own_rows.reshape(1, 3 * intersect_len)).astype(jnp.float32))

    def borrowed_rows(residue):
        requested = [
            lax.dot_general(
                selectors[col_off],
                residue,
                (((0,), (0,)), ((), ())),
                precision=HIGH,
                preferred_element_type=jnp.float32,
            ).reshape(3, intersect_len, rhs_count)
            for col_off in range(3)
        ]
        combined = jnp.stack([requested[col_off][1] for col_off in range(3)])
        for step_by, row_off in ((-1, 0), (1, 2)):
            outgoing = jnp.stack([requested[col_off][row_off] for col_off in range(3)])
            combined = combined + shifted(outgoing, "gx", step_by)
        gathered = combined[1]
        for step_by, col_off in ((-1, 0), (1, 2)):
            gathered = gathered + passed_along(combined[col_off], "gy", step_by)
        return gathered

    def precondition(residue):
        gathered = borrowed_rows(residue)
        extended = jnp.concatenate([residue, gathered], axis=0)
        solved = jnp.dot(inverse, extended, precision=HIGH, preferred_element_type=jnp.float32)
        returned = window_values(solved[points:])
        result = solved[:points]
        for col_off in range(3):
            result = result + jnp.dot(
                selectors[col_off],
                returned[col_off].reshape(3 * intersect_len, rhs_count),
                precision=HIGH,
                preferred_element_type=jnp.float32,
            )
        return result

    noise_col = own_noise[:, None]
    residual = right_side.reshape(points, rhs_count)
    solution = jnp.zeros_like(residual)
    precond = precondition(residual)
    direction = precond
    inner_now = residual_dot(residual, precond)
    for iteration in range(ITERS):
        columns = window_values(direction)
        accumulated = noise_col * direction
        for operate_row_off in range(3):
            for operate_col_off in range(3):
                accumulated = accumulated + jnp.dot(
                    kernel_block(own_pos, positions[operate_row_off][operate_col_off]),
                    columns[operate_col_off][operate_row_off],
                    precision=HIGH,
                    preferred_element_type=jnp.float32,
                )
        step_size = inner_now / lax.psum(column_sum(direction, accumulated), ("gx", "gy"))
        solution = solution + step_size * direction
        residual = residual - step_size * accumulated
        if iteration + 1 < ITERS:
            precond = precondition(residual)
            inner_next = residual_dot(residual, precond)
            direction = precond + inner_next / inner_now * direction
            inner_now = inner_next
    return (solution.reshape(1, 1, points, rhs_count), residual.reshape(1, 1, points, rhs_count))


def solution(mesh):
    placed = (
        P("gx", "gy", None, None),
        P("gx", "gy", None, None),
        P("gx", "gy", None),
        P("gx", "gy", None),
    )
    return jax.shard_map(
        shards,
        mesh=mesh,
        in_specs=placed,
        out_specs=(P("gx", "gy", None, None), P("gx", "gy", None, None)),
        check_vma=False,
    )
```

profile of v0, /device:TPU:0, one launch (start us, length us, event | category | flops | bytes accessed | tf_op | source)
XLA Modules:
  0.0 750.6 jit_solution(9324209336027450057)
XLA Ops:
  1.2 5.0 collective-permute-start.5
  7.0 4.4 collective-permute-start.1
  15.4 4.5 collective-permute-start.6
  23.5 3.7 collective-permute-start.2
  38.7 11.7 %cholesky.132 = f32[128,128]{1,0:T(8,128)S(1)} custom-call(f32[128,128]{1,0:T(8,128)S(1)} %cholesky.337), custom_call_target="Cholesky" | custom-call | tf_op jit(solution)/shard_map/jit(cholesky)/cholesky | solution.py:108
  50.6 9.8 %custom-call.38 = f32[1,128,128]{1,2,0:T(8,128)S(1)} custom-call(f32[1,128,128]{2,1,0:T(8,128)S(1)} %get-tuple-element.83), custom_call_target="InvertDiagBlocksLowerTriangular" | custom-call | tf_op jit(solution)/shard_map/jit(cholesky)/cholesky | solution.py:108
  63.0 11.9 %cholesky.270 = f32[128,128]{1,0:T(8,128)S(1)} custom-call(f32[128,128]{1,0:T(8,128)S(1)} %cholesky.341), custom_call_target="Cholesky" | custom-call | tf_op jit(solution)/shard_map/jit(cholesky)/cholesky | solution.py:108
  76.3 9.8 %custom-call.39 = f32[1,128,128]{1,2,0:T(8,128)S(1)} custom-call(f32[1,128,128]{2,1,0:T(8,128)S(1)} %get-tuple-element.80), custom_call_target="InvertDiagBlocksLowerTriangular" | custom-call | tf_op jit(solution)/shard_map/jit(cholesky)/cholesky | solution.py:108
  87.8 11.7 %cholesky.291 = f32[128,128]{1,0:T(8,128)S(1)} custom-call(f32[128,128]{1,0:T(8,128)S(1)} %cholesky.346), custom_call_target="Cholesky" | custom-call | tf_op jit(solution)/shard_map/jit(cholesky)/cholesky | solution.py:108
  100.3 9.8 %custom-call.40 = f32[1,128,128]{1,2,0:T(8,128)S(1)} custom-call(f32[1,128,128]{2,1,0:T(8,128)S(1)} %get-tuple-element.77), custom_call_target="InvertDiagBlocksLowerTriangular" | custom-call | tf_op jit(solution)/shard_map/jit(cholesky)/cholesky | solution.py:108
  112.0 11.7 %cholesky.310 = f32[128,128]{1,0:T(8,128)S(1)} custom-call(f32[128,128]{1,0:T(8,128)S(1)} %cholesky.351), custom_call_target="Cholesky" | custom-call | tf_op jit(solution)/shard_map/jit(cholesky)/cholesky | solution.py:108
  124.4 9.8 %custom-call.41 = f32[1,128,128]{1,2,0:T(8,128)S(1)} custom-call(f32[1,128,128]{2,1,0:T(8,128)S(1)} %get-tuple-element.74), custom_call_target="InvertDiagBlocksLowerTriangular" | custom-call | tf_op jit(solution)/shard_map/jit(cholesky)/cholesky | solution.py:108
  135.7 11.7 %cholesky.327 = f32[128,128]{1,0:T(8,128)S(1)} custom-call(f32[128,128]{1,0:T(8,128)S(1)} %convolution_subtract_fusion.6), custom_call_target="Cholesky" | custom-call | tf_op jit(solution)/shard_map/jit(cholesky)/cholesky | solution.py:108
  152.5 17.8 %while.1 = (s32[]{:T(128)}, f32[640,640]{1,0:T(8,128)}, s32[5,2]{0,1:T(2,128)S(1)}, f32[5,128,128]{2,1,0:T(8,128)}, s32[]{:T(128)}) while((s32[]{:T(128)}, f32[640,640]{1,0:T(8,128)}, s32[5,2]{0,1:T(2,128)S(1)}, f32[5,128,128]{2,1,0:T(8,128)}, s32[]{:T(128)}) %tuple.96), condition=%wide.while_cond, body=%wide.while_body.sunk | while | flops 2 | bytes 132705 | solution.py:109
  170.3 50.7 %custom-call.42 = f32[5,128,128]{1,2,0:T(8,128)} custom-call(f32[5,128,128]{2,1,0:T(8,128)} %get-tuple-element.10), custom_call_target="InvertDiagBlocksLowerTriangular" | custom-call | tf_op jit(solution)/shard_map/triangular_solve | solution.py:109
  234.1 4.7 collective-permute-start.11
  238.8 5.0 fusion.240
  245.7 4.4 collective-permute-start.13
  260.4 3.8 collective-permute-done.15
  264.9 4.4 collective-permute-start.17
  269.3 6.9 collective-permute-done.16
  285.3 26.6 %collective-permute-done.18 = f32[3,512,256]{2,1,0:T(8,128)S(1)} collective-permute-done((f32[3,512,256]{2,1,0:T(8,128)S(1)}, f32[3,512,256]{2,1,0:T(8,128)S(1)}, u32[]{:S(2)}, u32[]{:S(2)}) %collective-permute-start.18) | collective-permute-done | bytes 1572896 | tf_op jit(solution)/shard_map/ppermute | solution.py:21
  324.3 40.9 %all-reduce.1 = (f32[256]{0:T(256)S(1)}, f32[256]{0:T(256)S(1)}) all-reduce(f32[256]{0:T(256)S(1)} %get-tuple-element.12, f32[256]{0:T(256)S(1)} %get-tuple-element.11), channel_id=1, replica_groups=mesh['gx'=16,'gy'=2] {'gx','gy'}, use_global_device_ids=true, to_apply=%region_11.13 | all-reduce | flops 512 | bytes 4096 | tf_op jit(solution)/shard_map/psum | solution.py:61
  369.6 5.2 collective-permute-done.20
  374.7 4.8 collective-permute-done.21
  380.9 4.6 collective-permute-start.23
  391.3 4.1 collective-permute-start.25
  398.2 4.4 collective-permute-start.26
  404.5 7.1 collective-permute-done.26
  412.3 3.5 collective-permute-done.27
  417.2 36.8 %psum.44 = f32[256]{0:T(256)S(1)} all-reduce(f32[256]{0:T(256)S(1)} %get-tuple-element.128), channel_id=1, replica_groups=mesh['gx'=16,'gy'=2] {'gx','gy'}, use_global_device_ids=true, to_apply=%region_15.17 | all-reduce | flops 256 | bytes 2048 | tf_op jit(solution)/shard_map/psum | solution.py:61
  455.2 4.4 collective-permute-start.29
  459.6 7.0 collective-permute-done.28
  466.7 4.3 collective-permute-start.30
  478.3 24.6 %collective-permute-done.30 = f32[3,512,256]{2,1,0:T(8,128)S(1)} collective-permute-done((f32[3,512,256]{2,1,0:T(8,128)S(1)}, f32[3,512,256]{2,1,0:T(8,128)S(1)}, u32[]{:S(2)}, u32[]{:S(2)}) %collective-permute-start.30) | collective-permute-done | bytes 1572896 | tf_op jit(solution)/shard_map/ppermute | solution.py:21
  515.2 43.2 %psum.45 = f32[256]{0:T(256)S(1)} all-reduce(f32[256]{0:T(256)S(1)} %get-tuple-element.130), channel_id=1, replica_groups=mesh['gx'=16,'gy'=2] {'gx','gy'}, use_global_device_ids=true, to_apply=%region_17.19 | all-reduce | flops 256 | bytes 2048 | tf_op jit(solution)/shard_map/psum | solution.py:173
  562.8 5.2 collective-permute-done.32
  568.0 4.8 collective-permute-done.33
  574.2 4.6 collective-permute-start.35
  584.5 4.1 collective-permute-start.37
  591.4 4.4 collective-permute-start.38
  597.8 6.8 collective-permute-done.38
  609.4 36.9 %psum.46 = f32[256]{0:T(256)S(1)} all-reduce(f32[256]{0:T(256)S(1)} %get-tuple-element.132), channel_id=1, replica_groups=mesh['gx'=16,'gy'=2] {'gx','gy'}, use_global_device_ids=true, to_apply=%region_19.21 | all-reduce | flops 256 | bytes 2048 | tf_op jit(solution)/shard_map/psum | solution.py:61
  646.4 4.4 collective-permute-start.41
  650.8 7.0 collective-permute-done.40
  657.9 4.3 collective-permute-start.42
  669.3 25.0 %collective-permute-done.42 = f32[3,512,256]{2,1,0:T(8,128)S(1)} collective-permute-done((f32[3,512,256]{2,1,0:T(8,128)S(1)}, f32[3,512,256]{2,1,0:T(8,128)S(1)}, u32[]{:S(2)}, u32[]{:S(2)}) %collective-permute-start.42) | collective-permute-done | bytes 1572896 | tf_op jit(solution)/shard_map/ppermute | solution.py:21
  705.9 43.1 %psum.47 = f32[256]{0:T(256)S(1)} all-reduce(f32[256]{0:T(256)S(1)} %get-tuple-element.134), channel_id=1, replica_groups=mesh['gx'=16,'gy'=2] {'gx','gy'}, use_global_device_ids=true, to_apply=%region_21.23 | all-reduce | flops 256 | bytes 2048 | tf_op jit(solution)/shard_map/psum | solution.py:173
  (255 shorter events, 177.0 us)
Async XLA Ops:
  0.6 19.3 %copy-start = (f32[1,1,512,256]{3,2,1,0:T(8,128)S(1)}, f32[1,1,512,256]{3,2,1,0:T(8,128)}, u32[]{:S(2)}) copy-start(f32[1,1,512,256]{3,2,1,0:T(8,128)} %param.6) | copy-start | bytes 1572868
  0.7 13.4 %collective-permute-start.4 = (s32[128]{0:T(128)}, s32[128]{0:T(128)S(1)}, u32[]{:S(2)}, u32[]{:S(2)}) collective-permute-start(s32[128]{0:T(128)} %bitcast.373), channel_id=1, source_target_pairs={{0,2},{2,4},{4,6},{6,8},{8,10},{10,12},{12,14},{14,16},{16,18},{18... | collective-permute-start | bytes 1544 | tf_op jit(solution)/shard_map/ppermute | solution.py:15
  1.2 12.8 %collective-permute-start.5 = (s32[128]{0:T(128)}, s32[128]{0:T(128)S(1)}, u32[]{:S(2)}, u32[]{:S(2)}) collective-permute-start(s32[128]{0:T(128)} %bitcast.374), channel_id=1, source_target_pairs={{0,30},{2,0},{4,2},{6,4},{8,6},{10,8},{12,10},{14,12},{16,14},{18,... | collective-permute-start | bytes 1544 | tf_op jit(solution)/shard_map/ppermute | solution.py:15
  7.0 16.5 %collective-permute-start = (f32[3,512]{1,0:T(4,128)S(1)}, f32[3,512]{1,0:T(4,128)S(1)}, u32[]{:S(2)}, u32[]{:S(2)}) collective-permute-start(f32[3,512]{1,0:T(4,128)S(1)} %get-tuple-element.110), channel_id=1, source_target_pairs={{0,2},{2,4},{4,6},{6,8},{8,10},{10,12},{12,14},{14,16},{16,18},{18... | collective-permute-start | bytes 18440 | tf_op jit(solution)/shard_map/ppermute | solution.py:15
  7.0 16.4 %collective-permute-start.1 = (f32[3,512]{1,0:T(4,128)S(1)}, f32[3,512]{1,0:T(4,128)S(1)}, u32[]{:S(2)}, u32[]{:S(2)}) collective-permute-start(f32[3,512]{1,0:T(4,128)S(1)} %get-tuple-element.110), channel_id=1, source_target_pairs={{0,30},{2,0},{4,2},{6,4},{8,6},{10,8},{12,10},{14,12},{16,14},{18,... | collective-permute-start | bytes 18440 | tf_op jit(solution)/shard_map/ppermute | solution.py:15
  14.1 6.7 collective-permute-start.7
  15.4 6.3 collective-permute-start.6
  23.5 208.1 %collective-permute-start.8 = (f32[3,128,256]{2,1,0:T(8,128)}, f32[3,128,256]{2,1,0:T(8,128)}, u32[]{:S(2)}, u32[]{:S(2)}) collective-permute-start(f32[3,128,256]{2,1,0:T(8,128)} %pad_maximum_fusion.3), channel_id=1, source_target_pairs={{0,30},{2,0},{4,2},{6,4},{8,6},{10,8},{12,10},{14,12},{16,14},{18,... | collective-permute-start | bytes 1179656 | tf_op jit(solution)/shard_map/ppermute | solution.py:15
  23.5 7.5 collective-permute-start.2
  27.2 5.7 collective-permute-start.3
  29.3 202.3 %collective-permute-start.9 = (f32[3,128,256]{2,1,0:T(8,128)}, f32[3,128,256]{2,1,0:T(8,128)}, u32[]{:S(2)}, u32[]{:S(2)}) collective-permute-start(f32[3,128,256]{2,1,0:T(8,128)} %pad_maximum_fusion.4), channel_id=1, source_target_pairs={{0,2},{2,4},{4,6},{6,8},{8,10},{10,12},{12,14},{14,16},{16,18},{18... | collective-permute-start | bytes 1179656 | tf_op jit(solution)/shard_map/ppermute | solution.py:15
  170.3 54.7 %copy-start.3 = (f32[640,640]{1,0:T(8,128)S(1)}, f32[640,640]{1,0:T(8,128)}, u32[]{:S(2)}) copy-start(f32[640,640]{1,0:T(8,128)} %fusion.25) | copy-start | bytes 4915204
  232.8 11.1 %collective-permute-start.10 = (f32[128,256]{1,0:T(8,128)S(1)}, f32[128,256]{1,0:T(8,128)S(1)}, u32[]{:S(2)}, u32[]{:S(2)}) collective-permute-start(f32[128,256]{1,0:T(8,128)S(1)} %get-tuple-element.60), channel_id=1, source_target_pairs={{1,0},{3,2},{5,4},{7,6},{9,8},{11,10},{13,12},{15,14},{17,16},{19,... | collective-permute-start | bytes 393224 | tf_op jit(solution)/shard_map/ppermute | solution.py:21
  234.1 9.8 %collective-permute-start.11 = (f32[128,256]{1,0:T(8,128)S(1)}, f32[128,256]{1,0:T(8,128)S(1)}, u32[]{:S(2)}, u32[]{:S(2)}) collective-permute-start(f32[128,256]{1,0:T(8,128)S(1)} %get-tuple-element.61), channel_id=1, source_target_pairs={{0,1},{2,3},{4,5},{6,7},{8,9},{10,11},{12,13},{14,15},{16,17},{18,... | collective-permute-start | bytes 393224 | tf_op jit(solution)/shard_map/ppermute | solution.py:21
  245.7 7.1 collective-permute-start.12
  245.7 7.1 collective-permute-start.13
  252.9 6.9 collective-permute-start.14
  254.5 9.7 %collective-permute-start.15 = (f32[3,128,256]{2,1,0:T(8,128)S(1)}, f32[3,128,256]{2,1,0:T(8,128)S(1)}, u32[]{:S(2)}, u32[]{:S(2)}) collective-permute-start(f32[3,128,256]{2,1,0:T(8,128)S(1)} %pad_maximum_fusion.5), channel_id=1, source_target_pairs={{1,0},{3,2},{5,4},{7,6},{9,8},{11,10},{13,12},{15,14},{17,16},{19,... | collective-permute-start | bytes 1179656 | tf_op jit(solution)/shard_map/ppermute | solution.py:21
  264.8 11.5 %collective-permute-start.16 = (f32[512,256]{1,0:T(8,128)S(1)}, f32[512,256]{1,0:T(8,128)S(1)}, u32[]{:S(2)}, u32[]{:S(2)}) collective-permute-start(f32[512,256]{1,0:T(8,128)S(1)} %convolution_add_fusion.5), channel_id=1, source_target_pairs={{0,2},{2,4},{4,6},{6,8},{8,10},{10,12},{12,14},{14,16},{16,18},{18... | collective-permute-start | bytes 1572872 | tf_op jit(solution)/shard_map/ppermute | solution.py:15
  264.9 11.4 %collective-permute-start.17 = (f32[512,256]{1,0:T(8,128)S(1)}, f32[512,256]{1,0:T(8,128)S(1)}, u32[]{:S(2)}, u32[]{:S(2)}) collective-permute-start(f32[512,256]{1,0:T(8,128)S(1)} %convolution_add_fusion.5), channel_id=1, source_target_pairs={{0,30},{2,0},{4,2},{6,4},{8,6},{10,8},{12,10},{14,12},{16,14},{18,... | collective-permute-start | bytes 1572872 | tf_op jit(solution)/shard_map/ppermute | solution.py:15
  276.4 35.5 %collective-permute-start.18 = (f32[3,512,256]{2,1,0:T(8,128)S(1)}, f32[3,512,256]{2,1,0:T(8,128)S(1)}, u32[]{:S(2)}, u32[]{:S(2)}) collective-permute-start(f32[3,512,256]{2,1,0:T(8,128)S(1)} %pad_maximum_fusion), channel_id=1, source_target_pairs={{0,1},{2,3},{4,5},{6,7},{8,9},{10,11},{12,13},{14,15},{16,17},{18,... | collective-permute-start | bytes 4718600 | tf_op jit(solution)/shard_map/ppermute | solution.py:21
  278.0 39.5 %collective-permute-start.19 = (f32[3,512,256]{2,1,0:T(8,128)S(1)}, f32[3,512,256]{2,1,0:T(8,128)S(1)}, u32[]{:S(2)}, u32[]{:S(2)}) collective-permute-start(f32[3,512,256]{2,1,0:T(8,128)S(1)} %pad_maximum_fusion), channel_id=1, source_target_pairs={{1,0},{3,2},{5,4},{7,6},{9,8},{11,10},{13,12},{15,14},{17,16},{19,... | collective-permute-start | bytes 4718600 | tf_op jit(solution)/shard_map/ppermute | solution.py:21
  368.9 5.8 collective-permute-start.20
  369.5 10.1 %collective-permute-start.21 = (f32[3,128,256]{2,1,0:T(8,128)S(1)}, f32[3,128,256]{2,1,0:T(8,128)S(1)}, u32[]{:S(2)}, u32[]{:S(2)}) collective-permute-start(f32[3,128,256]{2,1,0:T(8,128)S(1)} %pad_maximum_fusion.7), channel_id=1, source_target_pairs={{0,2},{2,4},{4,6},{6,8},{8,10},{10,12},{12,14},{14,16},{16,18},{18... | collective-permute-start | bytes 1179656 | tf_op jit(solution)/shard_map/ppermute | solution.py:15
  379.6 7.7 %collective-permute-start.22 = (f32[128,256]{1,0:T(8,128)S(1)}, f32[128,256]{1,0:T(8,128)S(1)}, u32[]{:S(2)}, u32[]{:S(2)}) collective-permute-start(f32[128,256]{1,0:T(8,128)S(1)} %get-tuple-element.49), channel_id=1, source_target_pairs={{1,0},{3,2},{5,4},{7,6},{9,8},{11,10},{13,12},{15,14},{17,16},{19,... | collective-permute-start | bytes 393224 | tf_op jit(solution)/shard_map/ppermute | solution.py:21
  380.9 8.2 %collective-permute-start.23 = (f32[128,256]{1,0:T(8,128)S(1)}, f32[128,256]{1,0:T(8,128)S(1)}, u32[]{:S(2)}, u32[]{:S(2)}) collective-permute-start(f32[128,256]{1,0:T(8,128)S(1)} %get-tuple-element.50), channel_id=1, source_target_pairs={{0,1},{2,3},{4,5},{6,7},{8,9},{10,11},{12,13},{14,15},{16,17},{18,... | collective-permute-start | bytes 393224 | tf_op jit(solution)/shard_map/ppermute | solution.py:21
  390.9 7.2 collective-permute-start.24
  391.3 6.8 collective-permute-start.25
  398.2 13.5 %collective-permute-start.26 = (f32[3,128,256]{2,1,0:T(8,128)S(1)}, f32[3,128,256]{2,1,0:T(8,128)S(1)}, u32[]{:S(2)}, u32[]{:S(2)}) collective-permute-start(f32[3,128,256]{2,1,0:T(8,128)S(1)} %pad_maximum_fusion.8), channel_id=1, source_target_pairs={{0,1},{2,3},{4,5},{6,7},{8,9},{10,11},{12,13},{14,15},{16,17},{18,... | collective-permute-start | bytes 1179656 | tf_op jit(solution)/shard_map/ppermute | solution.py:21
  402.6 13.2 %collective-permute-start.27 = (f32[3,128,256]{2,1,0:T(8,128)S(1)}, f32[3,128,256]{2,1,0:T(8,128)S(1)}, u32[]{:S(2)}, u32[]{:S(2)}) collective-permute-start(f32[3,128,256]{2,1,0:T(8,128)S(1)} %pad_maximum_fusion.8), channel_id=1, source_target_pairs={{1,0},{3,2},{5,4},{7,6},{9,8},{11,10},{13,12},{15,14},{17,16},{19,... | collective-permute-start | bytes 1179656 | tf_op jit(solution)/shard_map/ppermute | solution.py:21
  455.1 57.2 %copy-start.1 = (f32[512,256]{1,0:T(8,128)}, f32[512,256]{1,0:T(8,128)S(1)}, u32[]{:S(2)}) copy-start(f32[512,256]{1,0:T(8,128)S(1)} %multiply_add_fusion.1) | copy-start | bytes 1572868
  455.1 11.5 %collective-permute-start.28 = (f32[512,256]{1,0:T(8,128)S(1)}, f32[512,256]{1,0:T(8,128)S(1)}, u32[]{:S(2)}, u32[]{:S(2)}) collective-permute-start(f32[512,256]{1,0:T(8,128)S(1)} %multiply_add_fusion.1), channel_id=1, source_target_pairs={{0,2},{2,4},{4,6},{6,8},{8,10},{10,12},{12,14},{14,16},{16,18},{18... | collective-permute-start | bytes 1572872 | tf_op jit(solution)/shard_map/ppermute | solution.py:15
  455.2 11.4 %collective-permute-start.29 = (f32[512,256]{1,0:T(8,128)S(1)}, f32[512,256]{1,0:T(8,128)S(1)}, u32[]{:S(2)}, u32[]{:S(2)}) collective-permute-start(f32[512,256]{1,0:T(8,128)S(1)} %multiply_add_fusion.1), channel_id=1, source_target_pairs={{0,30},{2,0},{4,2},{6,4},{8,6},{10,8},{12,10},{14,12},{16,14},{18,... | collective-permute-start | bytes 1572872 | tf_op jit(solution)/shard_map/ppermute | solution.py:15
  466.7 36.1 %collective-permute-start.30 = (f32[3,512,256]{2,1,0:T(8,128)S(1)}, f32[3,512,256]{2,1,0:T(8,128)S(1)}, u32[]{:S(2)}, u32[]{:S(2)}) collective-permute-start(f32[3,512,256]{2,1,0:T(8,128)S(1)} %pad_maximum_fusion.1), channel_id=1, source_target_pairs={{0,1},{2,3},{4,5},{6,7},{8,9},{10,11},{12,13},{14,15},{16,17},{18,... | collective-permute-start | bytes 4718600 | tf_op jit(solution)/shard_map/ppermute | solution.py:21
  471.0 37.4 %collective-permute-start.31 = (f32[3,512,256]{2,1,0:T(8,128)S(1)}, f32[3,512,256]{2,1,0:T(8,128)S(1)}, u32[]{:S(2)}, u32[]{:S(2)}) collective-permute-start(f32[3,512,256]{2,1,0:T(8,128)S(1)} %pad_maximum_fusion.1), channel_id=1, source_target_pairs={{1,0},{3,2},{5,4},{7,6},{9,8},{11,10},{13,12},{15,14},{17,16},{19,... | collective-permute-start | bytes 4718600 | tf_op jit(solution)/shard_map/ppermute | solution.py:21
  562.1 5.9 collective-permute-start.32
  562.7 10.1 %collective-permute-start.33 = (f32[3,128,256]{2,1,0:T(8,128)S(1)}, f32[3,128,256]{2,1,0:T(8,128)S(1)}, u32[]{:S(2)}, u32[]{:S(2)}) collective-permute-start(f32[3,128,256]{2,1,0:T(8,128)S(1)} %pad_maximum_fusion.10), channel_id=1, source_target_pairs={{0,2},{2,4},{4,6},{6,8},{8,10},{10,12},{12,14},{14,16},{16,18},{18... | collective-permute-start | bytes 1179656 | tf_op jit(solution)/shard_map/ppermute | solution.py:15
  572.9 7.8 %collective-permute-start.34 = (f32[128,256]{1,0:T(8,128)S(1)}, f32[128,256]{1,0:T(8,128)S(1)}, u32[]{:S(2)}, u32[]{:S(2)}) collective-permute-start(f32[128,256]{1,0:T(8,128)S(1)} %get-tuple-element.38), channel_id=1, source_target_pairs={{1,0},{3,2},{5,4},{7,6},{9,8},{11,10},{13,12},{15,14},{17,16},{19,... | collective-permute-start | bytes 393224 | tf_op jit(solution)/shard_map/ppermute | solution.py:21
  574.2 8.2 %collective-permute-start.35 = (f32[128,256]{1,0:T(8,128)S(1)}, f32[128,256]{1,0:T(8,128)S(1)}, u32[]{:S(2)}, u32[]{:S(2)}) collective-permute-start(f32[128,256]{1,0:T(8,128)S(1)} %get-tuple-element.39), channel_id=1, source_target_pairs={{0,1},{2,3},{4,5},{6,7},{8,9},{10,11},{12,13},{14,15},{16,17},{18,... | collective-permute-start | bytes 393224 | tf_op jit(solution)/shard_map/ppermute | solution.py:21
  584.2 7.2 collective-permute-start.36
  584.5 6.9 collective-permute-start.37
  591.4 13.1 %collective-permute-start.38 = (f32[3,128,256]{2,1,0:T(8,128)S(1)}, f32[3,128,256]{2,1,0:T(8,128)S(1)}, u32[]{:S(2)}, u32[]{:S(2)}) collective-permute-start(f32[3,128,256]{2,1,0:T(8,128)S(1)} %pad_maximum_fusion.11), channel_id=1, source_target_pairs={{0,1},{2,3},{4,5},{6,7},{8,9},{10,11},{12,13},{14,15},{16,17},{18,... | collective-permute-start | bytes 1179656 | tf_op jit(solution)/shard_map/ppermute | solution.py:21
  595.9 12.8 %collective-permute-start.39 = (f32[3,128,256]{2,1,0:T(8,128)S(1)}, f32[3,128,256]{2,1,0:T(8,128)S(1)}, u32[]{:S(2)}, u32[]{:S(2)}) collective-permute-start(f32[3,128,256]{2,1,0:T(8,128)S(1)} %pad_maximum_fusion.11), channel_id=1, source_target_pairs={{1,0},{3,2},{5,4},{7,6},{9,8},{11,10},{13,12},{15,14},{17,16},{19,... | collective-permute-start | bytes 1179656 | tf_op jit(solution)/shard_map/ppermute | solution.py:21
  605.2 41.1 %copy-start.2 = (f32[512,256]{1,0:T(8,128)S(1)}, f32[512,256]{1,0:T(8,128)}, u32[]{:S(2)}) copy-start(f32[512,256]{1,0:T(8,128)} %copy-done.1) | copy-start | bytes 1572868
  646.3 11.5 %collective-permute-start.40 = (f32[512,256]{1,0:T(8,128)S(1)}, f32[512,256]{1,0:T(8,128)S(1)}, u32[]{:S(2)}, u32[]{:S(2)}) collective-permute-start(f32[512,256]{1,0:T(8,128)S(1)} %multiply_add_fusion), channel_id=1, source_target_pairs={{0,2},{2,4},{4,6},{6,8},{8,10},{10,12},{12,14},{14,16},{16,18},{18... | collective-permute-start | bytes 1572872 | tf_op jit(solution)/shard_map/ppermute | solution.py:15
  646.4 11.4 %collective-permute-start.41 = (f32[512,256]{1,0:T(8,128)S(1)}, f32[512,256]{1,0:T(8,128)S(1)}, u32[]{:S(2)}, u32[]{:S(2)}) collective-permute-start(f32[512,256]{1,0:T(8,128)S(1)} %multiply_add_fusion), channel_id=1, source_target_pairs={{0,30},{2,0},{4,2},{6,4},{8,6},{10,8},{12,10},{14,12},{16,14},{18,... | collective-permute-start | bytes 1572872 | tf_op jit(solution)/shard_map/ppermute | solution.py:15
  657.9 36.3 %collective-permute-start.42 = (f32[3,512,256]{2,1,0:T(8,128)S(1)}, f32[3,512,256]{2,1,0:T(8,128)S(1)}, u32[]{:S(2)}, u32[]{:S(2)}) collective-permute-start(f32[3,512,256]{2,1,0:T(8,128)S(1)} %pad_maximum_fusion.2), channel_id=1, source_target_pairs={{0,1},{2,3},{4,5},{6,7},{8,9},{10,11},{12,13},{14,15},{16,17},{18,... | collective-permute-start | bytes 4718600 | tf_op jit(solution)/shard_map/ppermute | solution.py:21
  662.2 37.6 %collective-permute-start.43 = (f32[3,512,256]{2,1,0:T(8,128)S(1)}, f32[3,512,256]{2,1,0:T(8,128)S(1)}, u32[]{:S(2)}, u32[]{:S(2)}) collective-permute-start(f32[3,512,256]{2,1,0:T(8,128)S(1)} %pad_maximum_fusion.2), channel_id=1, source_target_pairs={{1,0},{3,2},{5,4},{7,6},{9,8},{11,10},{13,12},{15,14},{17,16},{19,... | collective-permute-start | bytes 4718600 | tf_op jit(solution)/shard_map/ppermute | solution.py:21
  (5 other events, 28.6 us)
where the time goes:
time: 756 us; the launch traced here: 751 us
  blocking collectives  201 us (27%)
  other arithmetic  168 us (22%)
  waiting for transfers between devices  161 us (21%)
  starting transfers between devices  96.9 us (13%)
  matrix products  94.8 us (13%)
  local copies, waits for them, and re-layouts  22.5 us (3%)
    psum x3, blocking collectives, residual_dot(): return lax.psum(column_sum(residue, precond), ('gx', 'gy'))  115 us
    ppermute x22, waiting for transfers between devices, passed_along(): return lax.ppermute(block, axis, route)  112 us
    another operation x19, other arithmetic, shards(): factor = jnp.linalg.cholesky(local_matrix)  101 us
    psum x2, blocking collectives, shards(): lax.psum(column_sum(direction, accumulated), ('gx', 'gy'))  86.3 us
    ppermute x22, starting transfers between devices, passed_along(): return lax.ppermute(block, axis, route)  57.9 us
    dot_general x27, matrix products, shards(): jnp.dot(kernel_block(own_pos, positions[operate_row_off][operate_col_off]...  52.9 us
    another operation x3, other arithmetic, shards(): lax.linalg.triangular_solve(factor, jnp.eye(ext_len, dtype=jnp.float32),...  52 us
    ppermute x22, waiting for transfers between devices, shifted(): lax.ppermute(value, axis, [(i, (i + by) % count) for i in range(count)])  49 us
  transfers between devices with their start and end apart: 44, of which 24 were waited for; matrix products, arithmetic and copies ran while one was open for 33% of the time, Pallas kernels for 0%

commit v1 on v0

--- a/solution.py
+++ b/solution.py
@@ -8,6 +8,10 @@
 RANGE_LEN = 0.25
 ROOT_THREE = math.sqrt(3.0)
 HIGH = lax.Precision.HIGHEST
+
+
+def unite_the_sector(w_in):
+    return lax.psum(lax.psum(w_in, axis_name="gy"), "gx")
 
 
 def shifted(value, axis, by):
@@ -170,7 +174,7 @@
                     precision=HIGH,
                     preferred_element_type=jnp.float32,
                 )
-        step_size = inner_now / lax.psum(column_sum(direction, accumulated), ("gx", "gy"))
+        step_size = inner_now / unite_the_sector(column_sum(direction, accumulated))
         solution = solution + step_size * direction
         residual = residual - step_size * accumulated
         if iteration + 1 < ITERS:

time: 756 us -> 777 us (1.028)
  blocking collectives: 201 us -> 229 us
  waiting for transfers between devices: 161 us -> 153 us
    psum x2 -> x6, blocking collectives: 86.3 us -> 116 us  [unite_the_sector(): return lax.psum(lax.psum(w_in, axis_name='gy'), 'gx')]
    ppermute x22, waiting for transfers between devices: 112 us -> 105 us  [passed_along(): return lax.ppermute(block, axis, route)]
  transfers between devices with their start and end apart: 44 -> 44, of which waited for: 24 -> 24; matrix products, arithmetic and copies ran while one was open for 33% -> 32% of each run, Pallas kernels for 0% -> 0%
where the time goes in v1:
time: 777 us; the launch traced here: 772 us
  blocking collectives  229 us (29%)
  other arithmetic  168 us (22%)
  waiting for transfers between devices  153 us (20%)
  starting transfers between devices  99.2 us (13%)
  matrix products  94.8 us (12%)
  local copies, waits for them, and re-layouts  22.7 us (3%)
    psum x6, blocking collectives, unite_the_sector(): return lax.psum(lax.psum(w_in, axis_name='gy'), 'gx')  116 us
    psum x3, blocking collectives, residual_dot(): return lax.psum(column_sum(residue, precond), ('gx', 'gy'))  113 us
    ppermute x22, waiting for transfers between devices, passed_along(): return lax.ppermute(block, axis, route)  105 us
    another operation x19, other arithmetic, shards(): factor = jnp.linalg.cholesky(local_matrix)  101 us
    ppermute x22, starting transfers between devices, passed_along(): return lax.ppermute(block, axis, route)  57.9 us
    dot_general x27, matrix products, shards(): jnp.dot(kernel_block(own_pos, positions[operate_row_off][operate_col_off]...  52.9 us
    another operation x3, other arithmetic, shards(): lax.linalg.triangular_solve(factor, jnp.eye(ext_len, dtype=jnp.float32),...  52 us
    ppermute x22, waiting for transfers between devices, shifted(): lax.ppermute(value, axis, [(i, (i + by) % count) for i in range(count)])  48.2 us
  transfers between devices with their start and end apart: 44, of which 24 were waited for; matrix products, arithmetic and copies ran while one was open for 32% of the time, Pallas kernels for 0%

profile of v1, /device:TPU:0, one launch (start us, length us, event | category | flops | bytes accessed | tf_op | source)
XLA Modules:
  0.0 772.3 jit_solution(13430832872647176282)
XLA Ops:
  1.2 5.0 collective-permute-start.5
  7.0 4.4 collective-permute-start.1
  15.4 4.5 collective-permute-start.6
  38.7 11.7 %cholesky.132 = f32[128,128]{1,0:T(8,128)S(1)} custom-call(f32[128,128]{1,0:T(8,128)S(1)} %cholesky.337), custom_call_target="Cholesky" | custom-call | tf_op jit(solution)/shard_map/jit(cholesky)/cholesky | solution.py:112
  50.5 9.8 %custom-call.38 = f32[1,128,128]{1,2,0:T(8,128)S(1)} custom-call(f32[1,128,128]{2,1,0:T(8,128)S(1)} %get-tuple-element.81), custom_call_target="InvertDiagBlocksLowerTriangular" | custom-call | tf_op jit(solution)/shard_map/jit(cholesky)/cholesky | solution.py:112
  63.0 11.9 %cholesky.270 = f32[128,128]{1,0:T(8,128)S(1)} custom-call(f32[128,128]{1,0:T(8,128)S(1)} %cholesky.341), custom_call_target="Cholesky" | custom-call | tf_op jit(solution)/shard_map/jit(cholesky)/cholesky | solution.py:112
  76.3 9.8 %custom-call.39 = f32[1,128,128]{1,2,0:T(8,128)S(1)} custom-call(f32[1,128,128]{2,1,0:T(8,128)S(1)} %get-tuple-element.78), custom_call_target="InvertDiagBlocksLowerTriangular" | custom-call | tf_op jit(solution)/shard_map/jit(cholesky)/cholesky | solution.py:112
  87.8 11.7 %cholesky.291 = f32[128,128]{1,0:T(8,128)S(1)} custom-call(f32[128,128]{1,0:T(8,128)S(1)} %cholesky.346), custom_call_target="Cholesky" | custom-call | tf_op jit(solution)/shard_map/jit(cholesky)/cholesky | solution.py:112
  100.2 9.8 %custom-call.40 = f32[1,128,128]{1,2,0:T(8,128)S(1)} custom-call(f32[1,128,128]{2,1,0:T(8,128)S(1)} %get-tuple-element.75), custom_call_target="InvertDiagBlocksLowerTriangular" | custom-call | tf_op jit(solution)/shard_map/jit(cholesky)/cholesky | solution.py:112
  111.9 11.7 %cholesky.310 = f32[128,128]{1,0:T(8,128)S(1)} custom-call(f32[128,128]{1,0:T(8,128)S(1)} %cholesky.351), custom_call_target="Cholesky" | custom-call | tf_op jit(solution)/shard_map/jit(cholesky)/cholesky | solution.py:112
  124.3 9.8 %custom-call.41 = f32[1,128,128]{1,2,0:T(8,128)S(1)} custom-call(f32[1,128,128]{2,1,0:T(8,128)S(1)} %get-tuple-element.72), custom_call_target="InvertDiagBlocksLowerTriangular" | custom-call | tf_op jit(solution)/shard_map/jit(cholesky)/cholesky | solution.py:112
  135.6 11.7 %cholesky.327 = f32[128,128]{1,0:T(8,128)S(1)} custom-call(f32[128,128]{1,0:T(8,128)S(1)} %convolution_subtract_fusion.6), custom_call_target="Cholesky" | custom-call | tf_op jit(solution)/shard_map/jit(cholesky)/cholesky | solution.py:112
  152.2 18.0 %while.1 = (s32[]{:T(128)}, f32[640,640]{1,0:T(8,128)}, s32[5,2]{0,1:T(2,128)S(1)}, f32[5,128,128]{2,1,0:T(8,128)}, s32[]{:T(128)}) while((s32[]{:T(128)}, f32[640,640]{1,0:T(8,128)}, s32[5,2]{0,1:T(2,128)S(1)}, f32[5,128,128]{2,1,0:T(8,128)}, s32[]{:T(128)}) %tuple.96), condition=%wide.while_cond, body=%wide.while_body.sunk | while | flops 2 | bytes 132705 | solution.py:113
  170.2 50.7 %custom-call.42 = f32[5,128,128]{1,2,0:T(8,128)} custom-call(f32[5,128,128]{2,1,0:T(8,128)} %get-tuple-element.10), custom_call_target="InvertDiagBlocksLowerTriangular" | custom-call | tf_op jit(solution)/shard_map/triangular_solve | solution.py:113
  234.0 4.7 collective-permute-start.11
  238.7 5.0 fusion.240
  245.6 4.4 collective-permute-start.13
  264.7 4.4 collective-permute-start.17
  269.2 6.9 collective-permute-done.16
  285.2 26.6 %collective-permute-done.18 = f32[3,512,256]{2,1,0:T(8,128)S(1)} collective-permute-done((f32[3,512,256]{2,1,0:T(8,128)S(1)}, f32[3,512,256]{2,1,0:T(8,128)S(1)}, u32[]{:S(2)}, u32[]{:S(2)}) %collective-permute-start.18) | collective-permute-done | bytes 1572896 | tf_op jit(solution)/shard_map/ppermute | solution.py:25
  324.1 5.4 psum.64
  329.5 32.1 %psum.65 = f32[256]{0:T(256)S(1)} all-reduce(f32[256]{0:T(256)S(1)} %psum.64), channel_id=1, replica_groups=mesh['gx'=16,'gy'=2] {'gx'}, use_global_device_ids=true, to_apply=%region_14.16 | all-reduce | flops 256 | bytes 2048 | tf_op jit(solution)/shard_map/psum | solution.py:14
  361.6 36.9 %psum.63 = f32[256]{0:T(256)S(1)} all-reduce(f32[256]{0:T(256)S(1)} %get-tuple-element.12), channel_id=1, replica_groups=mesh['gx'=16,'gy'=2] {'gx','gy'}, use_global_device_ids=true, to_apply=%region_11.13 | all-reduce | flops 256 | bytes 2048 | tf_op jit(solution)/shard_map/psum | solution.py:65
  405.2 5.2 collective-permute-done.20
  410.4 4.7 collective-permute-done.21
  416.4 4.6 collective-permute-start.23
  425.3 4.4 collective-permute-start.25
  432.5 4.4 collective-permute-start.26
  438.8 4.9 collective-permute-done.26
  449.2 39.0 %psum.66 = f32[256]{0:T(256)S(1)} all-reduce(f32[256]{0:T(256)S(1)} %get-tuple-element.126), channel_id=1, replica_groups=mesh['gx'=16,'gy'=2] {'gx','gy'}, use_global_device_ids=true, to_apply=%region_16.18 | all-reduce | flops 256 | bytes 2048 | tf_op jit(solution)/shard_map/psum | solution.py:65
  489.5 4.4 collective-permute-start.29
  493.9 7.0 collective-permute-done.28
  501.0 4.3 collective-permute-start.30
  512.6 23.4 %collective-permute-done.30 = f32[3,512,256]{2,1,0:T(8,128)S(1)} collective-permute-done((f32[3,512,256]{2,1,0:T(8,128)S(1)}, f32[3,512,256]{2,1,0:T(8,128)S(1)}, u32[]{:S(2)}, u32[]{:S(2)}) %collective-permute-start.30) | collective-permute-done | bytes 1572896 | tf_op jit(solution)/shard_map/ppermute | solution.py:25
  548.3 5.4 psum.67
  553.7 33.9 %psum.68 = f32[256]{0:T(256)S(1)} all-reduce(f32[256]{0:T(256)S(1)} %psum.67), channel_id=1, replica_groups=mesh['gx'=16,'gy'=2] {'gx'}, use_global_device_ids=true, to_apply=%region_19.21 | all-reduce | flops 256 | bytes 2048 | tf_op jit(solution)/shard_map/psum | solution.py:14
  592.0 4.7 collective-permute-done.32
  596.7 4.8 collective-permute-done.33
  602.9 4.6 collective-permute-start.35
  612.1 4.4 collective-permute-start.37
  619.2 4.4 collective-permute-start.38
  634.0 37.2 %psum.69 = f32[256]{0:T(256)S(1)} all-reduce(f32[256]{0:T(256)S(1)} %get-tuple-element.130), channel_id=1, replica_groups=mesh['gx'=16,'gy'=2] {'gx','gy'}, use_global_device_ids=true, to_apply=%region_21.23 | all-reduce | flops 256 | bytes 2048 | tf_op jit(solution)/shard_map/psum | solution.py:65
  671.4 4.4 collective-permute-start.41
  675.8 7.0 collective-permute-done.40
  682.9 4.3 collective-permute-start.42
  694.3 25.6 %collective-permute-done.42 = f32[3,512,256]{2,1,0:T(8,128)S(1)} collective-permute-done((f32[3,512,256]{2,1,0:T(8,128)S(1)}, f32[3,512,256]{2,1,0:T(8,128)S(1)}, u32[]{:S(2)}, u32[]{:S(2)}) %collective-permute-start.42) | collective-permute-done | bytes 1572896 | tf_op jit(solution)/shard_map/ppermute | solution.py:25
  731.5 5.4 psum.70
  736.9 33.8 %psum.71 = f32[256]{0:T(256)S(1)} all-reduce(f32[256]{0:T(256)S(1)} %psum.70), channel_id=1, replica_groups=mesh['gx'=16,'gy'=2] {'gx'}, use_global_device_ids=true, to_apply=%region_24.26 | all-reduce | flops 256 | bytes 2048 | tf_op jit(solution)/shard_map/psum | solution.py:14
  (259 shorter events, 191.2 us)
Async XLA Ops:
  0.6 19.3 %copy-start = (f32[1,1,512,256]{3,2,1,0:T(8,128)S(1)}, f32[1,1,512,256]{3,2,1,0:T(8,128)}, u32[]{:S(2)}) copy-start(f32[1,1,512,256]{3,2,1,0:T(8,128)} %param.6) | copy-start | bytes 1572868
  0.7 13.4 %collective-permute-start.4 = (s32[128]{0:T(128)}, s32[128]{0:T(128)S(1)}, u32[]{:S(2)}, u32[]{:S(2)}) collective-permute-start(s32[128]{0:T(128)} %bitcast.373), channel_id=1, source_target_pairs={{0,2},{2,4},{4,6},{6,8},{8,10},{10,12},{12,14},{14,16},{16,18},{18... | collective-permute-start | bytes 1544 | tf_op jit(solution)/shard_map/ppermute | solution.py:19
  1.2 12.8 %collective-permute-start.5 = (s32[128]{0:T(128)}, s32[128]{0:T(128)S(1)}, u32[]{:S(2)}, u32[]{:S(2)}) collective-permute-start(s32[128]{0:T(128)} %bitcast.374), channel_id=1, source_target_pairs={{0,30},{2,0},{4,2},{6,4},{8,6},{10,8},{12,10},{14,12},{16,14},{18,... | collective-permute-start | bytes 1544 | tf_op jit(solution)/shard_map/ppermute | solution.py:19
  7.0 16.5 %collective-permute-start = (f32[3,512]{1,0:T(4,128)S(1)}, f32[3,512]{1,0:T(4,128)S(1)}, u32[]{:S(2)}, u32[]{:S(2)}) collective-permute-start(f32[3,512]{1,0:T(4,128)S(1)} %get-tuple-element.108), channel_id=1, source_target_pairs={{0,2},{2,4},{4,6},{6,8},{8,10},{10,12},{12,14},{14,16},{16,18},{18... | collective-permute-start | bytes 18440 | tf_op jit(solution)/shard_map/ppermute | solution.py:19
  7.0 16.4 %collective-permute-start.1 = (f32[3,512]{1,0:T(4,128)S(1)}, f32[3,512]{1,0:T(4,128)S(1)}, u32[]{:S(2)}, u32[]{:S(2)}) collective-permute-start(f32[3,512]{1,0:T(4,128)S(1)} %get-tuple-element.108), channel_id=1, source_target_pairs={{0,30},{2,0},{4,2},{6,4},{8,6},{10,8},{12,10},{14,12},{16,14},{18,... | collective-permute-start | bytes 18440 | tf_op jit(solution)/shard_map/ppermute | solution.py:19
  14.1 6.7 collective-permute-start.7
  15.4 6.3 collective-permute-start.6
  23.4 208.0 %collective-permute-start.8 = (f32[3,128,256]{2,1,0:T(8,128)}, f32[3,128,256]{2,1,0:T(8,128)}, u32[]{:S(2)}, u32[]{:S(2)}) collective-permute-start(f32[3,128,256]{2,1,0:T(8,128)} %pad_maximum_fusion.3), channel_id=1, source_target_pairs={{0,30},{2,0},{4,2},{6,4},{8,6},{10,8},{12,10},{14,12},{16,14},{18,... | collective-permute-start | bytes 1179656 | tf_op jit(solution)/shard_map/ppermute | solution.py:19
  23.5 7.5 collective-permute-start.2
  27.2 5.7 collective-permute-start.3
  29.3 202.2 %collective-permute-start.9 = (f32[3,128,256]{2,1,0:T(8,128)}, f32[3,128,256]{2,1,0:T(8,128)}, u32[]{:S(2)}, u32[]{:S(2)}) collective-permute-start(f32[3,128,256]{2,1,0:T(8,128)} %pad_maximum_fusion.4), channel_id=1, source_target_pairs={{0,2},{2,4},{4,6},{6,8},{8,10},{10,12},{12,14},{14,16},{16,18},{18... | collective-permute-start | bytes 1179656 | tf_op jit(solution)/shard_map/ppermute | solution.py:19
  170.2 54.7 %copy-start.3 = (f32[640,640]{1,0:T(8,128)S(1)}, f32[640,640]{1,0:T(8,128)}, u32[]{:S(2)}) copy-start(f32[640,640]{1,0:T(8,128)} %fusion.25) | copy-start | bytes 4915204
  232.7 11.1 %collective-permute-start.10 = (f32[128,256]{1,0:T(8,128)S(1)}, f32[128,256]{1,0:T(8,128)S(1)}, u32[]{:S(2)}, u32[]{:S(2)}) collective-permute-start(f32[128,256]{1,0:T(8,128)S(1)} %get-tuple-element.58), channel_id=1, source_target_pairs={{1,0},{3,2},{5,4},{7,6},{9,8},{11,10},{13,12},{15,14},{17,16},{19,... | collective-permute-start | bytes 393224 | tf_op jit(solution)/shard_map/ppermute | solution.py:25
  234.0 9.8 %collective-permute-start.11 = (f32[128,256]{1,0:T(8,128)S(1)}, f32[128,256]{1,0:T(8,128)S(1)}, u32[]{:S(2)}, u32[]{:S(2)}) collective-permute-start(f32[128,256]{1,0:T(8,128)S(1)} %get-tuple-element.59), channel_id=1, source_target_pairs={{0,1},{2,3},{4,5},{6,7},{8,9},{10,11},{12,13},{14,15},{16,17},{18,... | collective-permute-start | bytes 393224 | tf_op jit(solution)/shard_map/ppermute | solution.py:25
  245.6 7.1 collective-permute-start.12
  245.6 7.1 collective-permute-start.13
  252.7 6.9 collective-permute-start.14
  254.4 9.7 %collective-permute-start.15 = (f32[3,128,256]{2,1,0:T(8,128)S(1)}, f32[3,128,256]{2,1,0:T(8,128)S(1)}, u32[]{:S(2)}, u32[]{:S(2)}) collective-permute-start(f32[3,128,256]{2,1,0:T(8,128)S(1)} %pad_maximum_fusion.5), channel_id=1, source_target_pairs={{1,0},{3,2},{5,4},{7,6},{9,8},{11,10},{13,12},{15,14},{17,16},{19,... | collective-permute-start | bytes 1179656 | tf_op jit(solution)/shard_map/ppermute | solution.py:25
  264.7 11.5 %collective-permute-start.16 = (f32[512,256]{1,0:T(8,128)S(1)}, f32[512,256]{1,0:T(8,128)S(1)}, u32[]{:S(2)}, u32[]{:S(2)}) collective-permute-start(f32[512,256]{1,0:T(8,128)S(1)} %convolution_add_fusion.5), channel_id=1, source_target_pairs={{0,2},{2,4},{4,6},{6,8},{8,10},{10,12},{12,14},{14,16},{16,18},{18... | collective-permute-start | bytes 1572872 | tf_op jit(solution)/shard_map/ppermute | solution.py:19
  264.7 11.4 %collective-permute-start.17 = (f32[512,256]{1,0:T(8,128)S(1)}, f32[512,256]{1,0:T(8,128)S(1)}, u32[]{:S(2)}, u32[]{:S(2)}) collective-permute-start(f32[512,256]{1,0:T(8,128)S(1)} %convolution_add_fusion.5), channel_id=1, source_target_pairs={{0,30},{2,0},{4,2},{6,4},{8,6},{10,8},{12,10},{14,12},{16,14},{18,... | collective-permute-start | bytes 1572872 | tf_op jit(solution)/shard_map/ppermute | solution.py:19
  276.3 35.5 %collective-permute-start.18 = (f32[3,512,256]{2,1,0:T(8,128)S(1)}, f32[3,512,256]{2,1,0:T(8,128)S(1)}, u32[]{:S(2)}, u32[]{:S(2)}) collective-permute-start(f32[3,512,256]{2,1,0:T(8,128)S(1)} %pad_maximum_fusion), channel_id=1, source_target_pairs={{0,1},{2,3},{4,5},{6,7},{8,9},{10,11},{12,13},{14,15},{16,17},{18,... | collective-permute-start | bytes 4718600 | tf_op jit(solution)/shard_map/ppermute | solution.py:25
  277.9 39.5 %collective-permute-start.19 = (f32[3,512,256]{2,1,0:T(8,128)S(1)}, f32[3,512,256]{2,1,0:T(8,128)S(1)}, u32[]{:S(2)}, u32[]{:S(2)}) collective-permute-start(f32[3,512,256]{2,1,0:T(8,128)S(1)} %pad_maximum_fusion), channel_id=1, source_target_pairs={{1,0},{3,2},{5,4},{7,6},{9,8},{11,10},{13,12},{15,14},{17,16},{19,... | collective-permute-start | bytes 4718600 | tf_op jit(solution)/shard_map/ppermute | solution.py:25
  402.1 8.2 %collective-permute-start.20 = (f32[3,128,256]{2,1,0:T(8,128)S(1)}, f32[3,128,256]{2,1,0:T(8,128)S(1)}, u32[]{:S(2)}, u32[]{:S(2)}) collective-permute-start(f32[3,128,256]{2,1,0:T(8,128)S(1)} %pad_maximum_fusion.6), channel_id=1, source_target_pairs={{0,30},{2,0},{4,2},{6,4},{8,6},{10,8},{12,10},{14,12},{16,14},{18,... | collective-permute-start | bytes 1179656 | tf_op jit(solution)/shard_map/ppermute | solution.py:19
  405.1 10.0 %collective-permute-start.21 = (f32[3,128,256]{2,1,0:T(8,128)S(1)}, f32[3,128,256]{2,1,0:T(8,128)S(1)}, u32[]{:S(2)}, u32[]{:S(2)}) collective-permute-start(f32[3,128,256]{2,1,0:T(8,128)S(1)} %pad_maximum_fusion.7), channel_id=1, source_target_pairs={{0,2},{2,4},{4,6},{6,8},{8,10},{10,12},{12,14},{14,16},{16,18},{18... | collective-permute-start | bytes 1179656 | tf_op jit(solution)/shard_map/ppermute | solution.py:19
  415.1 6.9 collective-permute-start.22
  416.4 7.1 collective-permute-start.23
  425.3 7.1 collective-permute-start.24
  425.3 7.1 collective-permute-start.25
  432.5 11.2 %collective-permute-start.26 = (f32[3,128,256]{2,1,0:T(8,128)S(1)}, f32[3,128,256]{2,1,0:T(8,128)S(1)}, u32[]{:S(2)}, u32[]{:S(2)}) collective-permute-start(f32[3,128,256]{2,1,0:T(8,128)S(1)} %pad_maximum_fusion.8), channel_id=1, source_target_pairs={{0,1},{2,3},{4,5},{6,7},{8,9},{10,11},{12,13},{14,15},{16,17},{18,... | collective-permute-start | bytes 1179656 | tf_op jit(solution)/shard_map/ppermute | solution.py:25
  436.8 11.0 %collective-permute-start.27 = (f32[3,128,256]{2,1,0:T(8,128)S(1)}, f32[3,128,256]{2,1,0:T(8,128)S(1)}, u32[]{:S(2)}, u32[]{:S(2)}) collective-permute-start(f32[3,128,256]{2,1,0:T(8,128)S(1)} %pad_maximum_fusion.8), channel_id=1, source_target_pairs={{1,0},{3,2},{5,4},{7,6},{9,8},{11,10},{13,12},{15,14},{17,16},{19,... | collective-permute-start | bytes 1179656 | tf_op jit(solution)/shard_map/ppermute | solution.py:25
  489.4 56.1 %copy-start.1 = (f32[512,256]{1,0:T(8,128)}, f32[512,256]{1,0:T(8,128)S(1)}, u32[]{:S(2)}) copy-start(f32[512,256]{1,0:T(8,128)S(1)} %multiply_add_fusion.1) | copy-start | bytes 1572868
  489.4 11.5 %collective-permute-start.28 = (f32[512,256]{1,0:T(8,128)S(1)}, f32[512,256]{1,0:T(8,128)S(1)}, u32[]{:S(2)}, u32[]{:S(2)}) collective-permute-start(f32[512,256]{1,0:T(8,128)S(1)} %multiply_add_fusion.1), channel_id=1, source_target_pairs={{0,2},{2,4},{4,6},{6,8},{8,10},{10,12},{12,14},{14,16},{16,18},{18... | collective-permute-start | bytes 1572872 | tf_op jit(solution)/shard_map/ppermute | solution.py:19
  489.5 11.4 %collective-permute-start.29 = (f32[512,256]{1,0:T(8,128)S(1)}, f32[512,256]{1,0:T(8,128)S(1)}, u32[]{:S(2)}, u32[]{:S(2)}) collective-permute-start(f32[512,256]{1,0:T(8,128)S(1)} %multiply_add_fusion.1), channel_id=1, source_target_pairs={{0,30},{2,0},{4,2},{6,4},{8,6},{10,8},{12,10},{14,12},{16,14},{18,... | collective-permute-start | bytes 1572872 | tf_op jit(solution)/shard_map/ppermute | solution.py:19
  501.0 35.0 %collective-permute-start.30 = (f32[3,512,256]{2,1,0:T(8,128)S(1)}, f32[3,512,256]{2,1,0:T(8,128)S(1)}, u32[]{:S(2)}, u32[]{:S(2)}) collective-permute-start(f32[3,512,256]{2,1,0:T(8,128)S(1)} %pad_maximum_fusion.1), channel_id=1, source_target_pairs={{0,1},{2,3},{4,5},{6,7},{8,9},{10,11},{12,13},{14,15},{16,17},{18,... | collective-permute-start | bytes 4718600 | tf_op jit(solution)/shard_map/ppermute | solution.py:25
  505.3 36.3 %collective-permute-start.31 = (f32[3,512,256]{2,1,0:T(8,128)S(1)}, f32[3,512,256]{2,1,0:T(8,128)S(1)}, u32[]{:S(2)}, u32[]{:S(2)}) collective-permute-start(f32[3,512,256]{2,1,0:T(8,128)S(1)} %pad_maximum_fusion.1), channel_id=1, source_target_pairs={{1,0},{3,2},{5,4},{7,6},{9,8},{11,10},{13,12},{15,14},{17,16},{19,... | collective-permute-start | bytes 4718600 | tf_op jit(solution)/shard_map/ppermute | solution.py:25
  591.3 5.4 collective-permute-start.32
  591.4 10.1 %collective-permute-start.33 = (f32[3,128,256]{2,1,0:T(8,128)S(1)}, f32[3,128,256]{2,1,0:T(8,128)S(1)}, u32[]{:S(2)}, u32[]{:S(2)}) collective-permute-start(f32[3,128,256]{2,1,0:T(8,128)S(1)} %pad_maximum_fusion.10), channel_id=1, source_target_pairs={{0,2},{2,4},{4,6},{6,8},{8,10},{10,12},{12,14},{14,16},{16,18},{18... | collective-permute-start | bytes 1179656 | tf_op jit(solution)/shard_map/ppermute | solution.py:19
  601.6 7.5 collective-permute-start.34
  602.9 7.4 collective-permute-start.35
  612.0 7.1 collective-permute-start.36
  612.1 7.1 collective-permute-start.37
  619.2 9.9 %collective-permute-start.38 = (f32[3,128,256]{2,1,0:T(8,128)S(1)}, f32[3,128,256]{2,1,0:T(8,128)S(1)}, u32[]{:S(2)}, u32[]{:S(2)}) collective-permute-start(f32[3,128,256]{2,1,0:T(8,128)S(1)} %pad_maximum_fusion.11), channel_id=1, source_target_pairs={{0,1},{2,3},{4,5},{6,7},{8,9},{10,11},{12,13},{14,15},{16,17},{18,... | collective-permute-start | bytes 1179656 | tf_op jit(solution)/shard_map/ppermute | solution.py:25
  623.6 9.7 %collective-permute-start.39 = (f32[3,128,256]{2,1,0:T(8,128)S(1)}, f32[3,128,256]{2,1,0:T(8,128)S(1)}, u32[]{:S(2)}, u32[]{:S(2)}) collective-permute-start(f32[3,128,256]{2,1,0:T(8,128)S(1)} %pad_maximum_fusion.11), channel_id=1, source_target_pairs={{1,0},{3,2},{5,4},{7,6},{9,8},{11,10},{13,12},{15,14},{17,16},{19,... | collective-permute-start | bytes 1179656 | tf_op jit(solution)/shard_map/ppermute | solution.py:25
  629.8 41.5 %copy-start.2 = (f32[512,256]{1,0:T(8,128)S(1)}, f32[512,256]{1,0:T(8,128)}, u32[]{:S(2)}) copy-start(f32[512,256]{1,0:T(8,128)} %copy-done.1) | copy-start | bytes 1572868
  671.3 11.5 %collective-permute-start.40 = (f32[512,256]{1,0:T(8,128)S(1)}, f32[512,256]{1,0:T(8,128)S(1)}, u32[]{:S(2)}, u32[]{:S(2)}) collective-permute-start(f32[512,256]{1,0:T(8,128)S(1)} %multiply_add_fusion), channel_id=1, source_target_pairs={{0,2},{2,4},{4,6},{6,8},{8,10},{10,12},{12,14},{14,16},{16,18},{18... | collective-permute-start | bytes 1572872 | tf_op jit(solution)/shard_map/ppermute | solution.py:19
  671.4 11.4 %collective-permute-start.41 = (f32[512,256]{1,0:T(8,128)S(1)}, f32[512,256]{1,0:T(8,128)S(1)}, u32[]{:S(2)}, u32[]{:S(2)}) collective-permute-start(f32[512,256]{1,0:T(8,128)S(1)} %multiply_add_fusion), channel_id=1, source_target_pairs={{0,30},{2,0},{4,2},{6,4},{8,6},{10,8},{12,10},{14,12},{16,14},{18,... | collective-permute-start | bytes 1572872 | tf_op jit(solution)/shard_map/ppermute | solution.py:19
  682.9 37.0 %collective-permute-start.42 = (f32[3,512,256]{2,1,0:T(8,128)S(1)}, f32[3,512,256]{2,1,0:T(8,128)S(1)}, u32[]{:S(2)}, u32[]{:S(2)}) collective-permute-start(f32[3,512,256]{2,1,0:T(8,128)S(1)} %pad_maximum_fusion.2), channel_id=1, source_target_pairs={{0,1},{2,3},{4,5},{6,7},{8,9},{10,11},{12,13},{14,15},{16,17},{18,... | collective-permute-start | bytes 4718600 | tf_op jit(solution)/shard_map/ppermute | solution.py:25
  687.2 38.3 %collective-permute-start.43 = (f32[3,512,256]{2,1,0:T(8,128)S(1)}, f32[3,512,256]{2,1,0:T(8,128)S(1)}, u32[]{:S(2)}, u32[]{:S(2)}) collective-permute-start(f32[3,512,256]{2,1,0:T(8,128)S(1)} %pad_maximum_fusion.2), channel_id=1, source_target_pairs={{1,0},{3,2},{5,4},{7,6},{9,8},{11,10},{13,12},{15,14},{17,16},{19,... | collective-permute-start | bytes 4718600 | tf_op jit(solution)/shard_map/ppermute | solution.py:25
  (5 other events, 28.5 us)
